TPU v7x, 32 devices: a whole 2x2x4 slice. The times are simulated.
32 devices in a mesh: rows: 8 (over z, y), feat: 4 (over x, core).
Axes of the slice: x: 2, y: 2, z: 4, core: 2. Of those that a mesh axis runs over, the one named last changes fastest.
Arguments:
- bin_index: int32 [16384, 512], P('rows', 'feat'), may hold values from 0 to 255
- leaf_ids: int32 [16384], P('rows'), may hold values from 0 to 15
- gradients: bfloat16 [16384], P('rows'), may hold values from -3 to 3
- hessians: bfloat16 [16384], P('rows'), may hold values from 0.049804688 to 0.25
Outputs:
- split_gains: float32 [4, 128, 16, 256], P('feat', 'rows')
- best_gain: float32 [16], replicated
All inputs are finite; a program needn't handle non-finite values.
Results may differ from a plain program's by a relative error of at most 0.0003.
Values may be sent and summed in bfloat16 or wider, within the bound.
A program may use at most 64 MiB of HBM per device.

v0:
```python
import math

import jax
import jax.numpy as jnp
from jax import lax
from jax.sharding import PartitionSpec as P

BINS = 256
LEAVES = 16


reg_lambda = 1.0


def gain_of(left_grad, left_hess):
    total_grad = left_grad[:, :, -1:]
    total_hess = left_hess[:, :, -1:]
    right_grad = total_grad - left_grad
    right_hess = total_hess - left_hess
    return 0.5 * (
        left_grad * left_grad / (left_hess + reg_lambda)
        + right_grad * right_grad / (right_hess + reg_lambda)
        - total_grad * total_grad / (total_hess + reg_lambda)
    )


def leaf_table(leaf_ids, gradients, hessians):
    members = leaf_ids[None, :] == jnp.arange(LEAVES, dtype=jnp.int32)[:, None]
    zero_value = jnp.zeros((), jnp.bfloat16)
    grad_part = jnp.where(members, gradients[None, :], zero_value)
    hess_part = jnp.where(members, hessians[None, :], zero_value)
    return jnp.concatenate([grad_part, hess_part], axis=0)


def partial_hist(weights, columns):
    onehot = (columns[:, :, None] == jnp.arange(BINS, dtype=jnp.int32)).astype(jnp.bfloat16)
    return jnp.einsum("cr,rfb->fcb", weights, onehot, preferred_element_type=jnp.float32)


def body(bin_index, leaf_ids, gradients, hessians):
    local_features = bin_index.shape[1]
    own_columns = local_features // lax.axis_size("rows")
    columns = lax.all_to_all(bin_index, "rows", split_axis=1, concat_axis=0, tiled=True)
    grad_pairs = jnp.stack([gradients, hessians], axis=0)
    all_pairs = lax.all_gather(grad_pairs, "rows", axis=1, tiled=True)
    all_leaves = lax.all_gather(leaf_ids, "rows", axis=0, tiled=True)
    total_rows = columns.shape[0]
    block_rows = math.gcd(total_rows, max(512, 16384 // own_columns))
    block_count = total_rows // block_rows

    def accumulate(running, position):
        first_row = position * block_rows
        part_columns = lax.dynamic_slice_in_dim(columns, first_row, block_rows, 0)
        part_pairs = lax.dynamic_slice_in_dim(all_pairs, first_row, block_rows, 1)
        part_leaves = lax.dynamic_slice_in_dim(all_leaves, first_row, block_rows, 0)
        weights = leaf_table(part_leaves, part_pairs[0], part_pairs[1])
        return (running + partial_hist(weights, part_columns), None)

    initial = jnp.zeros((own_columns, 2 * LEAVES, BINS), jnp.float32)
    totals, unused = lax.scan(accumulate, initial, jnp.arange(block_count, dtype=jnp.int32))
    left_sums = jnp.cumsum(totals, axis=2)
    split_gains = gain_of(left_sums[:, :LEAVES], left_sums[:, LEAVES:])
    best_gain = lax.pmax(jnp.max(split_gains, axis=(0, 2)), ("rows", "feat"))
    return (split_gains[None], best_gain)


def solution(mesh):
    placed = (P("rows", "feat"), P("rows"), P("rows"), P("rows"))
    return jax.shard_map(
        body,
        mesh=mesh,
        in_specs=placed,
        out_specs=(P("feat", "rows", None, None), P()),
        check_vma=False,
    )
```

profile of v0, /device:TPU:0, one launch (start us, length us, event | category | flops | bytes accessed | tf_op | source)
XLA Modules:
  0.0 212.5 jit_solution(15374470001416995448)
XLA Ops:
  0.6 2.6 %copy.19 = s32[2048,128]{0,1:T(8,128)} copy(s32[2048,128]{1,0:T(8,128)} %param.6) | data formatting | bytes 2097152 | tf_op args[0]
  3.2 7.4 %all-to-all-start = ((s32[2048,8,16]{0,2,1:T(8,128)}), s32[2048,8,16]{0,2,1:T(8,128)S(1)}, u32[]{:S(2)}, u32[]{:S(2)}) async-start(s32[2048,8,16]{0,2,1:T(8,128)} %bitcast), calls=%async_computation | async-start | bytes 2097152 | tf_op jit(solution)/shard_map/all_to_all | solution.py:43
  10.7 45.7 %all_gather.7 = bf16[2,16384]{1,0:T(2,128)(2,1)S(1)} all-gather(bf16[2,2048]{1,0:T(2,128)(2,1)S(1)} %pad_maximum_fusion), channel_id=1, replica_groups=mesh['rows'=8,'feat'=4] {'rows'}, dimensions={1}, use_global_device_ids=true | all-gather | bytes 73728 | tf_op jit(solution)/shard_map/all_gather | solution.py:45
  56.4 30.5 %all_gather.6 = s32[16384]{0:T(1024)S(1)} all-gather(s32[2048]{0:T(1024)S(1)} %copy-done), channel_id=1, replica_groups=mesh['rows'=8,'feat'=4] {'rows'}, dimensions={0}, use_global_device_ids=true | all-gather | bytes 73728 | tf_op jit(solution)/shard_map/all_gather | solution.py:46
  87.1 76.4 %while.11 = (s32[]{:T(128)}, f32[16,32,256]{2,1,0:T(8,128)S(1)}, s32[16]{0:T(128)S(1)}, s32[16384,16]{0,1:T(8,128)S(1)}, s32[16384]{0:T(1024)S(1)}, /*index=5*/b...) while((s32[]{:T(128)}, f32[16,32,256]{2,1,0:T(8,128)S(1)}, ...), condition=%wide.region_1.2_spmd.clone, body=%wide.region_0.1_spmd.clone.sunk | while | flops 273072128 | bytes 1401037 | solution.py:60
  88.5 3.3 %fusion.17 = f32[16,32,256]{2,1,0:T(8,128)S(1)} fusion(s32[1024,16]{0,1:T(8,128)S(1)} %constant_dynamic-slice_fusion.2, f32[16,32,256]{2,1,0:T(8,128)S(1)} %get-tuple-element.134, pred[]{:T(512)S(6)} %compare.3, bf16[16,1024]{1,0:T(8,128)(2,1)S(1)} %get-tuple-element.120, bf16[16,1024]{1,0:T(8,128)(2,1)S(1)} %get-tuple-element.121), kind=kOutput, calls=%fused_computation.4.clone.1 | convolution fusion | flops 273022976 | bytes 1179649 | tf_op jit(solution)/shard_map/while/body/eval_jaxpr/cr,rfb->fcb/dot_general | solution.py:37
  93.3 3.3 %fusion.17 = f32[16,32,256]{2,1,0:T(8,128)S(1)} fusion(s32[1024,16]{0,1:T(8,128)S(1)} %constant_dynamic-slice_fusion.2, f32[16,32,256]{2,1,0:T(8,128)S(1)} %get-tuple-element.134, pred[]{:T(512)S(6)} %compare.3, bf16[16,1024]{1,0:T(8,128)(2,1)S(1)} %get-tuple-element.120, bf16[16,1024]{1,0:T(8,128)(2,1)S(1)} %get-tuple-element.121), kind=kOutput, calls=%fused_computation.4.clone.1 | convolution fusion | flops 273022976 | bytes 1179649 | tf_op jit(solution)/shard_map/while/body/eval_jaxpr/cr,rfb->fcb/dot_general | solution.py:37
  98.1 3.3 %fusion.17 = f32[16,32,256]{2,1,0:T(8,128)S(1)} fusion(s32[1024,16]{0,1:T(8,128)S(1)} %constant_dynamic-slice_fusion.2, f32[16,32,256]{2,1,0:T(8,128)S(1)} %get-tuple-element.134, pred[]{:T(512)S(6)} %compare.3, bf16[16,1024]{1,0:T(8,128)(2,1)S(1)} %get-tuple-element.120, bf16[16,1024]{1,0:T(8,128)(2,1)S(1)} %get-tuple-element.121), kind=kOutput, calls=%fused_computation.4.clone.1 | convolution fusion | flops 273022976 | bytes 1179649 | tf_op jit(solution)/shard_map/while/body/eval_jaxpr/cr,rfb->fcb/dot_general | solution.py:37
  102.8 3.3 %fusion.17 = f32[16,32,256]{2,1,0:T(8,128)S(1)} fusion(s32[1024,16]{0,1:T(8,128)S(1)} %constant_dynamic-slice_fusion.2, f32[16,32,256]{2,1,0:T(8,128)S(1)} %get-tuple-element.134, pred[]{:T(512)S(6)} %compare.3, bf16[16,1024]{1,0:T(8,128)(2,1)S(1)} %get-tuple-element.120, bf16[16,1024]{1,0:T(8,128)(2,1)S(1)} %get-tuple-element.121), kind=kOutput, calls=%fused_computation.4.clone.1 | convolution fusion | flops 273022976 | bytes 1179649 | tf_op jit(solution)/shard_map/while/body/eval_jaxpr/cr,rfb->fcb/dot_general | solution.py:37
  107.6 3.3 %fusion.17 = f32[16,32,256]{2,1,0:T(8,128)S(1)} fusion(s32[1024,16]{0,1:T(8,128)S(1)} %constant_dynamic-slice_fusion.2, f32[16,32,256]{2,1,0:T(8,128)S(1)} %get-tuple-element.134, pred[]{:T(512)S(6)} %compare.3, bf16[16,1024]{1,0:T(8,128)(2,1)S(1)} %get-tuple-element.120, bf16[16,1024]{1,0:T(8,128)(2,1)S(1)} %get-tuple-element.121), kind=kOutput, calls=%fused_computation.4.clone.1 | convolution fusion | flops 273022976 | bytes 1179649 | tf_op jit(solution)/shard_map/while/body/eval_jaxpr/cr,rfb->fcb/dot_general | solution.py:37
  112.4 3.3 %fusion.17 = f32[16,32,256]{2,1,0:T(8,128)S(1)} fusion(s32[1024,16]{0,1:T(8,128)S(1)} %constant_dynamic-slice_fusion.2, f32[16,32,256]{2,1,0:T(8,128)S(1)} %get-tuple-element.134, pred[]{:T(512)S(6)} %compare.3, bf16[16,1024]{1,0:T(8,128)(2,1)S(1)} %get-tuple-element.120, bf16[16,1024]{1,0:T(8,128)(2,1)S(1)} %get-tuple-element.121), kind=kOutput, calls=%fused_computation.4.clone.1 | convolution fusion | flops 273022976 | bytes 1179649 | tf_op jit(solution)/shard_map/while/body/eval_jaxpr/cr,rfb->fcb/dot_general | solution.py:37
  117.1 3.3 %fusion.17 = f32[16,32,256]{2,1,0:T(8,128)S(1)} fusion(s32[1024,16]{0,1:T(8,128)S(1)} %constant_dynamic-slice_fusion.2, f32[16,32,256]{2,1,0:T(8,128)S(1)} %get-tuple-element.134, pred[]{:T(512)S(6)} %compare.3, bf16[16,1024]{1,0:T(8,128)(2,1)S(1)} %get-tuple-element.120, bf16[16,1024]{1,0:T(8,128)(2,1)S(1)} %get-tuple-element.121), kind=kOutput, calls=%fused_computation.4.clone.1 | convolution fusion | flops 273022976 | bytes 1179649 | tf_op jit(solution)/shard_map/while/body/eval_jaxpr/cr,rfb->fcb/dot_general | solution.py:37
  121.9 3.3 %fusion.17 = f32[16,32,256]{2,1,0:T(8,128)S(1)} fusion(s32[1024,16]{0,1:T(8,128)S(1)} %constant_dynamic-slice_fusion.2, f32[16,32,256]{2,1,0:T(8,128)S(1)} %get-tuple-element.134, pred[]{:T(512)S(6)} %compare.3, bf16[16,1024]{1,0:T(8,128)(2,1)S(1)} %get-tuple-element.120, bf16[16,1024]{1,0:T(8,128)(2,1)S(1)} %get-tuple-element.121), kind=kOutput, calls=%fused_computation.4.clone.1 | convolution fusion | flops 273022976 | bytes 1179649 | tf_op jit(solution)/shard_map/while/body/eval_jaxpr/cr,rfb->fcb/dot_general | solution.py:37
  126.7 3.3 %fusion.17 = f32[16,32,256]{2,1,0:T(8,128)S(1)} fusion(s32[1024,16]{0,1:T(8,128)S(1)} %constant_dynamic-slice_fusion.2, f32[16,32,256]{2,1,0:T(8,128)S(1)} %get-tuple-element.134, pred[]{:T(512)S(6)} %compare.3, bf16[16,1024]{1,0:T(8,128)(2,1)S(1)} %get-tuple-element.120, bf16[16,1024]{1,0:T(8,128)(2,1)S(1)} %get-tuple-element.121), kind=kOutput, calls=%fused_computation.4.clone.1 | convolution fusion | flops 273022976 | bytes 1179649 | tf_op jit(solution)/shard_map/while/body/eval_jaxpr/cr,rfb->fcb/dot_general | solution.py:37
  131.5 3.3 %fusion.17 = f32[16,32,256]{2,1,0:T(8,128)S(1)} fusion(s32[1024,16]{0,1:T(8,128)S(1)} %constant_dynamic-slice_fusion.2, f32[16,32,256]{2,1,0:T(8,128)S(1)} %get-tuple-element.134, pred[]{:T(512)S(6)} %compare.3, bf16[16,1024]{1,0:T(8,128)(2,1)S(1)} %get-tuple-element.120, bf16[16,1024]{1,0:T(8,128)(2,1)S(1)} %get-tuple-element.121), kind=kOutput, calls=%fused_computation.4.clone.1 | convolution fusion | flops 273022976 | bytes 1179649 | tf_op jit(solution)/shard_map/while/body/eval_jaxpr/cr,rfb->fcb/dot_general | solution.py:37
  136.2 3.3 %fusion.17 = f32[16,32,256]{2,1,0:T(8,128)S(1)} fusion(s32[1024,16]{0,1:T(8,128)S(1)} %constant_dynamic-slice_fusion.2, f32[16,32,256]{2,1,0:T(8,128)S(1)} %get-tuple-element.134, pred[]{:T(512)S(6)} %compare.3, bf16[16,1024]{1,0:T(8,128)(2,1)S(1)} %get-tuple-element.120, bf16[16,1024]{1,0:T(8,128)(2,1)S(1)} %get-tuple-element.121), kind=kOutput, calls=%fused_computation.4.clone.1 | convolution fusion | flops 273022976 | bytes 1179649 | tf_op jit(solution)/shard_map/while/body/eval_jaxpr/cr,rfb->fcb/dot_general | solution.py:37
  141.0 3.3 %fusion.17 = f32[16,32,256]{2,1,0:T(8,128)S(1)} fusion(s32[1024,16]{0,1:T(8,128)S(1)} %constant_dynamic-slice_fusion.2, f32[16,32,256]{2,1,0:T(8,128)S(1)} %get-tuple-element.134, pred[]{:T(512)S(6)} %compare.3, bf16[16,1024]{1,0:T(8,128)(2,1)S(1)} %get-tuple-element.120, bf16[16,1024]{1,0:T(8,128)(2,1)S(1)} %get-tuple-element.121), kind=kOutput, calls=%fused_computation.4.clone.1 | convolution fusion | flops 273022976 | bytes 1179649 | tf_op jit(solution)/shard_map/while/body/eval_jaxpr/cr,rfb->fcb/dot_general | solution.py:37
  145.8 3.3 %fusion.17 = f32[16,32,256]{2,1,0:T(8,128)S(1)} fusion(s32[1024,16]{0,1:T(8,128)S(1)} %constant_dynamic-slice_fusion.2, f32[16,32,256]{2,1,0:T(8,128)S(1)} %get-tuple-element.134, pred[]{:T(512)S(6)} %compare.3, bf16[16,1024]{1,0:T(8,128)(2,1)S(1)} %get-tuple-element.120, bf16[16,1024]{1,0:T(8,128)(2,1)S(1)} %get-tuple-element.121), kind=kOutput, calls=%fused_computation.4.clone.1 | convolution fusion | flops 273022976 | bytes 1179649 | tf_op jit(solution)/shard_map/while/body/eval_jaxpr/cr,rfb->fcb/dot_general | solution.py:37
  150.6 3.3 %fusion.17 = f32[16,32,256]{2,1,0:T(8,128)S(1)} fusion(s32[1024,16]{0,1:T(8,128)S(1)} %constant_dynamic-slice_fusion.2, f32[16,32,256]{2,1,0:T(8,128)S(1)} %get-tuple-element.134, pred[]{:T(512)S(6)} %compare.3, bf16[16,1024]{1,0:T(8,128)(2,1)S(1)} %get-tuple-element.120, bf16[16,1024]{1,0:T(8,128)(2,1)S(1)} %get-tuple-element.121), kind=kOutput, calls=%fused_computation.4.clone.1 | convolution fusion | flops 273022976 | bytes 1179649 | tf_op jit(solution)/shard_map/while/body/eval_jaxpr/cr,rfb->fcb/dot_general | solution.py:37
  155.3 3.3 %fusion.17 = f32[16,32,256]{2,1,0:T(8,128)S(1)} fusion(s32[1024,16]{0,1:T(8,128)S(1)} %constant_dynamic-slice_fusion.2, f32[16,32,256]{2,1,0:T(8,128)S(1)} %get-tuple-element.134, pred[]{:T(512)S(6)} %compare.3, bf16[16,1024]{1,0:T(8,128)(2,1)S(1)} %get-tuple-element.120, bf16[16,1024]{1,0:T(8,128)(2,1)S(1)} %get-tuple-element.121), kind=kOutput, calls=%fused_computation.4.clone.1 | convolution fusion | flops 273022976 | bytes 1179649 | tf_op jit(solution)/shard_map/while/body/eval_jaxpr/cr,rfb->fcb/dot_general | solution.py:37
  160.1 3.3 %fusion.17 = f32[16,32,256]{2,1,0:T(8,128)S(1)} fusion(s32[1024,16]{0,1:T(8,128)S(1)} %constant_dynamic-slice_fusion.2, f32[16,32,256]{2,1,0:T(8,128)S(1)} %get-tuple-element.134, pred[]{:T(512)S(6)} %compare.3, bf16[16,1024]{1,0:T(8,128)(2,1)S(1)} %get-tuple-element.120, bf16[16,1024]{1,0:T(8,128)(2,1)S(1)} %get-tuple-element.121), kind=kOutput, calls=%fused_computation.4.clone.1 | convolution fusion | flops 273022976 | bytes 1179649 | tf_op jit(solution)/shard_map/while/body/eval_jaxpr/cr,rfb->fcb/dot_general | solution.py:37
  163.5 9.2 %reduce-window.6 = f32[16,32,2,128]{3,1,2,0:T(8,128)S(1)} reduce-window(f32[16,32,2,128]{3,1,2,0:T(8,128)S(1)} %copy_bitcast_fusion.1, f32[]{:T(128)} %constant.18.clone.1), window={size=1x1x1x128 pad=0_0x0_0x0_0x127_0}, to_apply=%region_2.3 | reduce-window | flops 16646144 | bytes 1048580 | tf_op jit(solution)/shard_map/reduce-window
  173.8 1.0 fusion.12
  174.8 37.7 %pmax.7 = f32[16]{0:T(128)} all-reduce(f32[16]{0:T(128)S(1)} %get-tuple-element.73), channel_id=1, replica_groups=mesh['rows'=8,'feat'=4] {'rows','feat'}, use_global_device_ids=true, to_apply=%region_5.6 | all-reduce | flops 16 | bytes 128 | tf_op jit(solution)/shard_map/pmax | solution.py:63
  (101 shorter events, 12.8 us)
Async XLA Ops:
  3.2 7.5 %copy-start.1 = (bf16[2048]{0:T(1024)(128)(2,1)S(1)}, bf16[2048]{0:T(1024)(128)(2,1)}, u32[]{:S(2)}) copy-start(bf16[2048]{0:T(1024)(128)(2,1)} %param.9) | copy-start | bytes 12292
  3.2 7.5 %copy-start.2 = (bf16[2048]{0:T(1024)(128)(2,1)S(1)}, bf16[2048]{0:T(1024)(128)(2,1)}, u32[]{:S(2)}) copy-start(bf16[2048]{0:T(1024)(128)(2,1)} %param.8) | copy-start | bytes 12292
  3.2 53.3 %copy-start = (s32[2048]{0:T(1024)S(1)}, s32[2048]{0:T(1024)}, u32[]{:S(2)}) copy-start(s32[2048]{0:T(1024)} %param.7) | copy-start | bytes 24580
  3.2 83.8 %all-to-all-start = ((s32[2048,8,16]{0,2,1:T(8,128)}), s32[2048,8,16]{0,2,1:T(8,128)S(1)}, u32[]{:S(2)}, u32[]{:S(2)}) async-start(s32[2048,8,16]{0,2,1:T(8,128)} %bitcast), calls=%async_computation | async-start | bytes 2097152 | tf_op jit(solution)/shard_map/all_to_all | solution.py:43
where the time goes:
time: 213 us
  blocking collectives  114 us (54%)
  matrix products  53.4 us (25%)
  local copies, waits for them, and re-layouts  14.6 us (7%)
  loops' own time  11.3 us (5%)
  other arithmetic  11.1 us (5%)
  starting transfers between devices  7.44 us (3%)
    dot_general x16, matrix products, partial_hist(): jnp.einsum('cr,rfb->fcb', weights, onehot, preferred_element_type=jnp.flo...  53.4 us
    all_gather x1, blocking collectives, body(): all_pairs = lax.all_gather(grad_pairs, 'rows', axis=1, tiled=True)  45.7 us
    pmax x1, blocking collectives, body(): best_gain = lax.pmax(jnp.max(split_gains, axis=(0, 2)), ('rows', 'feat'))  37.7 us
    all_gather x1, blocking collectives, body(): all_leaves = lax.all_gather(leaf_ids, 'rows', axis=0, tiled=True)  30.5 us
    another operation x1, loops' own time, body(): lax.scan(accumulate, initial, jnp.arange(block_count, dtype=jnp.int32))  11.3 us
    another operation x3, other arithmetic  9.5 us
    dynamic_slice x16, local copies, waits for them, and re-layouts, body(): lax.scan(accumulate, initial, jnp.arange(block_count, dtype=jnp.int32))  9.38 us
    all_to_all x1, starting transfers between devices, body(): lax.all_to_all(bin_index, 'rows', split_axis=1, concat_axis=0, tiled=True)  7.44 us
  transfers between devices with their start and end apart: 1, of which 0 were waited for; matrix products, arithmetic and copies ran while one was open for 0% of the time, Pallas kernels for 0%

commit v1 on v0

v1 whole, which is shorter than its diff:
```python
import functools

import jax
import jax.numpy as jnp
from jax import lax
from jax.experimental import pallas as pl
from jax.experimental.pallas import tpu as pltpu
from jax.sharding import PartitionSpec as P

BINS = 256
LEAVES = 16
LANES = 128
HALF = BINS // 2
MESH = pl.DeviceIdType.MESH

reg_lambda = 1.0


def max_exchange(axis, count, source, landing, send_sems, recv_sems):
    me = lax.axis_index(axis)

    def copy_to(step):
        return pltpu.make_async_remote_copy(
            src_ref=source,
            dst_ref=landing.at[me],
            send_sem=send_sems.at[step],
            recv_sem=recv_sems.at[me],
            device_id={axis: lax.rem(me + step, count)},
            device_id_type=MESH,
        )

    def copy_from(step):
        origin = lax.rem(me - step + count, count)
        return origin, pltpu.make_async_remote_copy(
            src_ref=source,
            dst_ref=landing.at[origin],
            send_sem=send_sems.at[step],
            recv_sem=recv_sems.at[origin],
            device_id={axis: origin},
            device_id_type=MESH,
        )

    def start(step, carry):
        copy_to(step).start()
        return carry

    def collect(step, largest):
        origin, copy = copy_from(step)
        copy.wait_recv()
        return jnp.maximum(largest, landing[origin])

    def finish(step, carry):
        copy_to(step).wait_send()
        return carry

    lax.fori_loop(1, count, start, 0)
    largest = lax.fori_loop(1, count, collect, source[...])
    lax.fori_loop(1, count, finish, 0)
    return largest


def kernel(n, n_feat, group, bins_ref, meta_ref, gain_ref, best_ref, columns, metas, weights, sums,
           top_rows, top_feat, land_rows, land_feat,
           bin_send, bin_recv, meta_send, meta_recv, own_sems,
           row_send, row_recv, feat_send, feat_recv):
    me = lax.axis_index("rows")
    me_feat = lax.axis_index("feat")
    own, rows = bins_ref.shape[1], bins_ref.shape[2]
    tiles = rows // LANES

    barrier = pltpu.get_barrier_semaphore()

    def greet_rows(step, carry):
        pl.semaphore_signal(barrier, inc=1, device_id={"rows": lax.rem(me + step, n)}, device_id_type=MESH)
        return carry

    def greet_feat(step, carry):
        pl.semaphore_signal(barrier, inc=1, device_id={"feat": lax.rem(me_feat + step, n_feat)}, device_id_type=MESH)
        return carry

    lax.fori_loop(1, n, greet_rows, 0)
    lax.fori_loop(1, n_feat, greet_feat, 0)
    own_bins = pltpu.make_async_copy(bins_ref.at[me], columns.at[me], own_sems.at[0])
    own_meta = pltpu.make_async_copy(meta_ref, metas.at[me], own_sems.at[1])
    own_bins.start()
    own_meta.start()
    pl.semaphore_wait(barrier, n - 1 + n_feat - 1)

    def send(step):
        target = lax.rem(me + step, n)
        bins_copy = pltpu.make_async_remote_copy(
            src_ref=bins_ref.at[target], dst_ref=columns.at[me], send_sem=bin_send.at[step],
            recv_sem=bin_recv.at[me], device_id={"rows": target}, device_id_type=MESH)
        meta_copy = pltpu.make_async_remote_copy(
            src_ref=meta_ref, dst_ref=metas.at[me], send_sem=meta_send.at[step],
            recv_sem=meta_recv.at[me], device_id={"rows": target}, device_id_type=MESH)
        return bins_copy, meta_copy

    def receive(step):
        origin = lax.rem(me - step + n, n)
        bins_copy = pltpu.make_async_remote_copy(
            src_ref=bins_ref.at[origin], dst_ref=columns.at[origin], send_sem=bin_send.at[step],
            recv_sem=bin_recv.at[origin], device_id={"rows": origin}, device_id_type=MESH)
        meta_copy = pltpu.make_async_remote_copy(
            src_ref=meta_ref, dst_ref=metas.at[origin], send_sem=meta_send.at[step],
            recv_sem=meta_recv.at[origin], device_id={"rows": origin}, device_id_type=MESH)
        return bins_copy, meta_copy

    def start_sends(step, carry):
        for copy in send(step):
            copy.start()
        return carry

    lax.fori_loop(1, n, start_sends, 0)
    sums[...] = jnp.zeros_like(sums)
    own_bins.wait()
    own_meta.wait()

    def one_shard(step, carry):
        origin = lax.rem(me - step + n, n)

        @pl.when(step > 0)
        def arrived():
            for copy in receive(step):
                copy.wait_recv()

        table = metas[origin].astype(jnp.float32)
        leaf_of = lax.broadcasted_iota(jnp.int32, (LEAVES, LANES), 0).astype(jnp.float32)
        for tile in range(tiles):
            member = jnp.broadcast_to(table[tile:tile + 1], (LEAVES, LANES)) == leaf_of
            for part in (0, 1):
                first = (1 + part) * tiles + tile
                value = jnp.broadcast_to(table[first:first + 1], (LEAVES, LANES))
                weights[part * LEAVES:(part + 1) * LEAVES, tile * LANES:(tile + 1) * LANES] = (
                    jnp.where(member, value, 0.0).astype(jnp.bfloat16))

        block = columns[origin]
        level = lax.broadcasted_iota(jnp.int32, (HALF, rows), 0).astype(jnp.bfloat16)
        one, zero = jnp.ones((), jnp.bfloat16), jnp.zeros((), jnp.bfloat16)
        table_rows = weights[...]
        for first in range(0, own, group):
            left_side, right_side = [], []
            for feature in range(first, first + group):
                bins = block[feature:feature + 1]
                upper = bins >= HALF
                low = jnp.where(upper, bins - HALF, bins)
                upper_wide = jnp.broadcast_to(bins, (2 * LEAVES, rows)) >= HALF
                left_side.append(jnp.where(upper_wide, zero, table_rows))
                left_side.append(jnp.where(upper_wide, table_rows, zero))
                right_side.append(jnp.where(jnp.broadcast_to(low, (HALF, rows)) <= level, one, zero))
            product = lax.dot_general(
                jnp.concatenate(left_side, axis=0), jnp.concatenate(right_side, axis=0),
                (((1,), (1,)), ((), ())), preferred_element_type=jnp.float32)
            for place in range(group):
                sums[first + place] += product[place * 4 * LEAVES:(place + 1) * 4 * LEAVES, place * HALF:(place + 1) * HALF]
        return carry

    lax.fori_loop(0, n, one_shard, 0)

    def finish_sends(step, carry):
        for copy in send(step):
            copy.wait_send()
        return carry

    lax.fori_loop(1, n, finish_sends, 0)

    def gains(feature, largest):
        part = sums[feature]
        grad_low, hess_low = part[:LEAVES], part[LEAVES:2 * LEAVES]
        grad_high = part[2 * LEAVES:3 * LEAVES] + grad_low[:, HALF - 1:]
        hess_high = part[3 * LEAVES:] + hess_low[:, HALF - 1:]
        total_grad, total_hess = grad_high[:, HALF - 1:], hess_high[:, HALF - 1:]
        whole = total_grad * total_grad / (total_hess + reg_lambda)
        for place, left_grad, left_hess in ((0, grad_low, hess_low), (1, grad_high, hess_high)):
            right_grad, right_hess = total_grad - left_grad, total_hess - left_hess
            gain = 0.5 * (left_grad * left_grad / (left_hess + reg_lambda)
                          + right_grad * right_grad / (right_hess + reg_lambda) - whole)
            gain_ref[feature, :, place * HALF:(place + 1) * HALF] = gain
            largest = jnp.maximum(largest, gain)
        return largest

    top_rows[...] = lax.fori_loop(0, own, gains, jnp.full((LEAVES, HALF), -jnp.inf, jnp.float32))
    top_feat[...] = max_exchange("rows", n, top_rows, land_rows, row_send, row_recv)
    largest = max_exchange("feat", n_feat, top_feat, land_feat, feat_send, feat_recv)
    best_ref[...] = jnp.broadcast_to(jnp.max(largest, axis=1, keepdims=True), best_ref.shape)


def body(bin_index, leaf_ids, gradients, hessians):
    n, n_feat = lax.axis_size("rows"), lax.axis_size("feat")
    rows, local_features = bin_index.shape
    own = local_features // n
    group = 2 if own % 2 == 0 else 1
    bins = bin_index.T.astype(jnp.bfloat16).reshape(n, own, rows)
    meta = jnp.concatenate([leaf_ids.astype(jnp.bfloat16), gradients, hessians]).reshape(3 * rows // LANES, LANES)
    vmem = pl.BlockSpec(memory_space=pltpu.VMEM)
    dma = pltpu.SemaphoreType.DMA
    gain, best = pl.pallas_call(
        functools.partial(kernel, n, n_feat, group),
        out_shape=(jax.ShapeDtypeStruct((own, LEAVES, BINS), jnp.float32),
                   jax.ShapeDtypeStruct((LEAVES, LANES), jnp.float32)),
        in_specs=[vmem, vmem],
        out_specs=(vmem, vmem),
        scratch_shapes=[
            pltpu.VMEM((n, own, rows), jnp.bfloat16),
            pltpu.VMEM((n,) + meta.shape, jnp.bfloat16),
            pltpu.VMEM((2 * LEAVES, rows), jnp.bfloat16),
            pltpu.VMEM((own, 4 * LEAVES, HALF), jnp.float32),
            pltpu.VMEM((LEAVES, HALF), jnp.float32),
            pltpu.VMEM((LEAVES, HALF), jnp.float32),
            pltpu.VMEM((n, LEAVES, HALF), jnp.float32),
            pltpu.VMEM((n_feat, LEAVES, HALF), jnp.float32),
            dma((n,)), dma((n,)), dma((n,)), dma((n,)), dma((2,)),
            dma((n,)), dma((n,)), dma((n_feat,)), dma((n_feat,)),
        ],
        compiler_params=pltpu.CompilerParams(
            collective_id=0, has_side_effects=True, vmem_limit_bytes=60 * 1024 * 1024),
    )(bins, meta)
    return gain[None], best[:, 0]


def solution(mesh):
    placed = (P("rows", "feat"), P("rows"), P("rows"), P("rows"))
    return jax.shard_map(
        body,
        mesh=mesh,
        in_specs=placed,
        out_specs=(P("feat", "rows", None, None), P()),
        check_vma=False,
    )
```

time: 213 us -> 54 us (0.25)
  blocking collectives: 114 us -> 0 us
  matrix products: 53.4 us -> 0 us
  Pallas kernels: 0 us -> 46.5 us
  loops' own time: 11.3 us -> 0 us
  local copies, waits for them, and re-layouts: 14.6 us -> 4.69 us
  other arithmetic: 11.1 us -> 1.88 us
  starting transfers between devices: 7.44 us -> 0 us
    all_gather x2 -> x0, blocking collectives: 76.3 us -> none  [the longest x1 45.7 us: body(): all_pairs = lax.all_gather(grad_pairs, 'rows', axis=1, tiled=True)]
    dot_general x16 -> x0, matrix products: 53.4 us -> none  [partial_hist(): jnp.einsum('cr,rfb->fcb', weights, onehot, preferred_element_type=jnp.flo...]
    pallas_call x0 -> x1, Pallas kernels: none -> 46.5 us  [body(): pl.pallas_call(functools.partial(kernel, n, n_feat, group), out_shape=(ja...]
    pmax x1 -> x0, blocking collectives: 37.7 us -> none  [body(): best_gain = lax.pmax(jnp.max(split_gains, axis=(0, 2)), ('rows', 'feat'))]
    another operation x1 -> x0, loops' own time: 11.3 us -> none  [body(): lax.scan(accumulate, initial, jnp.arange(block_count, dtype=jnp.int32))]
    dynamic_slice x48 -> x0, local copies, waits for them, and re-layouts: 9.73 us -> none  [the longest x16 9.38 us: body(): lax.scan(accumulate, initial, jnp.arange(block_count, dtype=jnp.int32))]
    another operation x4 -> x0, other arithmetic: 9.53 us -> none
    all_to_all x1 -> x0, starting transfers between devices: 7.44 us -> none  [body(): lax.all_to_all(bin_index, 'rows', split_axis=1, concat_axis=0, tiled=True)]
  transfers between devices with their start and end apart: 1 -> 0, of which waited for: 0 -> 0; matrix products, arithmetic and copies ran while one was open for 0% -> 0% of each run, Pallas kernels for 0% -> 0%
where the time goes in v1:
time: 54 us; the launch traced here: 53.7 us
  Pallas kernels  46.5 us (86%)
  local copies, waits for them, and re-layouts  4.69 us (9%)
  other arithmetic  1.88 us (3%)
  between operations  0.65 us (1%)
    pallas_call x1, Pallas kernels, body(): pl.pallas_call(functools.partial(kernel, n, n_feat, group), out_shape=(ja...  46.5 us
    unnamed x7, local copies, waits for them, and re-layouts  2.37 us
    slice x1, local copies, waits for them, and re-layouts, body(): return (gain[None], best[:, 0])  1.32 us
    convert_element_type x1, other arithmetic, body(): bins = bin_index.T.astype(jnp.bfloat16).reshape(n, own, rows)  1.28 us

profile of v1, /device:TPU:0, one launch (start us, length us, event | category | flops | bytes accessed | tf_op | source)
XLA Modules:
  0.0 53.7 jit_solution(1104350941582489988)
XLA Ops:
  0.6 1.3 %convert_bitcast_fusion = bf16[128,2048]{0,1:T(8,128)(2,1)S(1)} fusion(s32[2048,128]{1,0:T(8,128)} %param.4), kind=kLoop, calls=%fused_computation | loop fusion | flops 262144 | bytes 1572864 | tf_op jit(solution)/shard_map/convert_element_type | solution.py:193
  1.9 0.0 copy-start
  1.9 1.0 %copy.7 = bf16[128,2048]{1,0:T(8,128)(2,1)} copy(bf16[128,2048]{0,1:T(8,128)(2,1)S(1)} %convert_bitcast_fusion) | data formatting | bytes 1048576 | tf_op jit(solution)/shard_map/convert_element_type | solution.py:193
  2.9 0.0 copy-done
  2.9 0.0 copy-start.1
  2.9 0.0 copy-start.2
  2.9 0.7 %copy-done.1 = bf16[2048]{0:T(1024)(128)(2,1)S(1)} copy-done((bf16[2048]{0:T(1024)(128)(2,1)S(1)}, bf16[2048]{0:T(1024)(128)(2,1)}, u32[]{:S(2)}) %copy-start.1) | copy-done | bytes 4120
  3.6 0.0 copy-done.2
  3.6 0.6 %pad_maximum_fusion.meta_ref = bf16[48,128]{1,0:T(8,128)(2,1)} fusion(bf16[16,128]{1,0:T(8,128)(2,1)S(1)} %bitcast.10, bf16[16,128]{1,0:T(8,128)(2,1)S(1)} %bitcast.11, bf16[16,128]{1,0:T(8,128)(2,1)S(1)} %convert_bitcast_fusion.1), kind=kLoop, calls=%fused_computation.1 | loop fusion | flops 36864 | bytes 24576 | tf_op jit(solution)/shard_map/concatenate | solution.py:194
  4.2 46.5 %shard_map.59 = (f32[16,16,256]{2,1,0:T(8,128)}, f32[16,128]{1,0:T(8,128)}) custom-call(bf16[8,16,2048]{2,1,0:T(8,128)(2,1)} %bitcast.8, bf16[48,128]{1,0:T(8,128)(2,1)} %pad_maximum_fusion.meta_ref), custom_call_target="tpu_custom_call" | custom-call | tf_op jit(solution)/shard_map/pallas_call | solution.py:197
  50.7 1.3 %slice_reduce_fusion = f32[16]{0:T(128)} fusion(f32[16,128]{1,0:T(8,128)} %get-tuple-element.5), kind=kLoop, calls=%fused_computation.2 | loop fusion | bytes 128 | tf_op jit(solution)/shard_map/slice | solution.py:218
  52.1 1.7 %copy.9 = f32[1,16,16,256]{3,2,1,0:T(8,128)} copy(f32[1,16,16,256]{3,2,1,0:T(8,128)} %bitcast.9) | data formatting | bytes 524288
  (1 shorter events, 0.0 us)
Async XLA Ops:
  1.9 1.0 %copy-start = (s32[2048]{0:T(1024)S(1)}, s32[2048]{0:T(1024)}, u32[]{:S(2)}) copy-start(s32[2048]{0:T(1024)} %param.5) | copy-start | bytes 24580
  2.9 0.7 %copy-start.1 = (bf16[2048]{0:T(1024)(128)(2,1)S(1)}, bf16[2048]{0:T(1024)(128)(2,1)}, u32[]{:S(2)}) copy-start(bf16[2048]{0:T(1024)(128)(2,1)} %param.7) | copy-start | bytes 12292
  2.9 0.7 %copy-start.2 = (bf16[2048]{0:T(1024)(128)(2,1)S(1)}, bf16[2048]{0:T(1024)(128)(2,1)}, u32[]{:S(2)}) copy-start(bf16[2048]{0:T(1024)(128)(2,1)} %param.6) | copy-start | bytes 12292

commit v2 on v1

v2 whole, which is shorter than its diff:
```python
import functools

import jax
import jax.numpy as jnp
from jax import lax
from jax.experimental import pallas as pl
from jax.experimental.pallas import tpu as pltpu
from jax.sharding import PartitionSpec as P

BINS = 256
LEAVES = 16
LANES = 128
HALF = BINS // 2
MESH = pl.DeviceIdType.MESH

reg_lambda = 1.0


def kernel(n, n_feat, group, bins_hbm, leaf_ref, grad_ref, hess_ref, gain_ref, best_ref,
           raw, bins_src, meta_src, columns, metas, weights, sums, top, landing,
           raw_sems, bin_send, bin_recv, meta_send, meta_recv, own_sems, top_send, top_recv):
    me, me_feat = lax.axis_index("rows"), lax.axis_index("feat")
    everyone = n * n_feat
    me_all = me * n_feat + me_feat
    own, rows = bins_src.shape[1], bins_src.shape[2]
    tiles = rows // LANES
    pieces = raw_sems.shape[0]
    piece_rows = rows // pieces

    def fetch(piece):
        span = pl.ds(piece * piece_rows, piece_rows)
        return pltpu.make_async_copy(bins_hbm.at[span], raw.at[span], raw_sems.at[piece])

    for piece in range(pieces):
        fetch(piece).start()

    def device_after(step):
        other = lax.rem(me_all + step, everyone)
        return {"rows": other // n_feat, "feat": lax.rem(other, n_feat)}

    barrier = pltpu.get_barrier_semaphore()

    def greet(step, carry):
        pl.semaphore_signal(barrier, inc=1, device_id=device_after(step), device_id_type=MESH)
        return carry

    lax.fori_loop(1, everyone, greet, 0)

    meta_src[:tiles] = leaf_ref[...].astype(jnp.float32).astype(jnp.bfloat16)
    meta_src[tiles:2 * tiles] = grad_ref[...]
    meta_src[2 * tiles:] = hess_ref[...]
    for piece in range(pieces):
        fetch(piece).wait()
        for tile in range(piece * piece_rows // LANES, (piece + 1) * piece_rows // LANES):
            lanes = slice(tile * LANES, (tile + 1) * LANES)
            turned = raw[lanes].astype(jnp.float32).T.astype(jnp.bfloat16)
            bins_src[:, :, lanes] = turned.reshape(n, own, LANES)

    own_bins = pltpu.make_async_copy(bins_src.at[me], columns.at[me], own_sems.at[0])
    own_meta = pltpu.make_async_copy(meta_src, metas.at[me], own_sems.at[1])
    own_bins.start()
    own_meta.start()
    pl.semaphore_wait(barrier, everyone - 1)

    def partner(step):
        other, bit = 0, 1
        while bit < n:
            other += lax.rem(me // bit + step // bit, 2) * bit
            bit *= 2
        return other

    def exchange(step, landed):
        other = partner(step)
        place = other if landed else me
        copies = []
        for source, target, send_sems, recv_sems in (
                (meta_src, metas, meta_send, meta_recv), (bins_src.at[other], columns, bin_send, bin_recv)):
            copies.append(pltpu.make_async_remote_copy(
                src_ref=source, dst_ref=target.at[place], send_sem=send_sems.at[step],
                recv_sem=recv_sems.at[step], device_id={"rows": other}, device_id_type=MESH))
        return copies

    def start_sends(step, carry):
        for copy in exchange(step, False):
            copy.start()
        return carry

    lax.fori_loop(1, n, start_sends, 0)
    sums[...] = jnp.zeros_like(sums)
    own_bins.wait()
    own_meta.wait()

    def one_shard(step, carry):
        origin = partner(step)

        @pl.when(step > 0)
        def arrived():
            for copy in exchange(step, True):
                copy.wait_recv()

        table = metas[origin].astype(jnp.float32)
        leaf_of = lax.broadcasted_iota(jnp.int32, (LEAVES, LANES), 0).astype(jnp.float32)
        for tile in range(tiles):
            member = jnp.broadcast_to(table[tile:tile + 1], (LEAVES, LANES)) == leaf_of
            for part in (0, 1):
                first = (1 + part) * tiles + tile
                value = jnp.broadcast_to(table[first:first + 1], (LEAVES, LANES))
                weights[part * LEAVES:(part + 1) * LEAVES, tile * LANES:(tile + 1) * LANES] = (
                    jnp.where(member, value, 0.0).astype(jnp.bfloat16))

        block = columns[origin]
        level = lax.broadcasted_iota(jnp.int32, (HALF, rows), 0).astype(jnp.bfloat16)
        one, zero = jnp.ones((), jnp.bfloat16), jnp.zeros((), jnp.bfloat16)
        table_rows = weights[...]
        for first in range(0, own, group):
            left_side, right_side = [], []
            for feature in range(first, first + group):
                bins = block[feature:feature + 1]
                upper = bins >= HALF
                low = jnp.where(upper, bins - HALF, bins)
                upper_wide = jnp.broadcast_to(bins, (2 * LEAVES, rows)) >= HALF
                left_side.append(jnp.where(upper_wide, zero, table_rows))
                left_side.append(jnp.where(upper_wide, table_rows, zero))
                right_side.append(jnp.where(jnp.broadcast_to(low, (HALF, rows)) <= level, one, zero))
            product = lax.dot_general(
                jnp.concatenate(left_side, axis=0), jnp.concatenate(right_side, axis=0),
                (((1,), (1,)), ((), ())), preferred_element_type=jnp.float32)
            for place in range(group):
                sums[first + place] += product[place * 4 * LEAVES:(place + 1) * 4 * LEAVES, place * HALF:(place + 1) * HALF]
        return carry

    lax.fori_loop(0, n, one_shard, 0)

    def gains(feature, largest):
        part = sums[feature]
        grad_low, hess_low = part[:LEAVES], part[LEAVES:2 * LEAVES]
        grad_high = part[2 * LEAVES:3 * LEAVES] + grad_low[:, HALF - 1:]
        hess_high = part[3 * LEAVES:] + hess_low[:, HALF - 1:]
        total_grad, total_hess = grad_high[:, HALF - 1:], hess_high[:, HALF - 1:]
        whole = total_grad * total_grad / (total_hess + reg_lambda)
        for place, left_grad, left_hess in ((0, grad_low, hess_low), (1, grad_high, hess_high)):
            right_grad, right_hess = total_grad - left_grad, total_hess - left_hess
            gain = 0.5 * (left_grad * left_grad / (left_hess + reg_lambda)
                          + right_grad * right_grad / (right_hess + reg_lambda) - whole)
            gain_ref[feature, :, place * HALF:(place + 1) * HALF] = gain
            largest = jnp.maximum(largest, gain)
        return largest

    largest = lax.fori_loop(0, own, gains, jnp.full((LEAVES, HALF), -jnp.inf, jnp.float32))
    largest = jnp.broadcast_to(jnp.max(largest, axis=1, keepdims=True), (LEAVES, LANES))
    on_lane = (lax.broadcasted_iota(jnp.int32, (LEAVES, LANES), 0) == lax.broadcasted_iota(jnp.int32, (LEAVES, LANES), 1))
    top[...] = jnp.max(jnp.where(on_lane, largest, -jnp.inf), axis=0, keepdims=True)

    def report(step):
        return pltpu.make_async_remote_copy(
            src_ref=top, dst_ref=landing.at[step], send_sem=top_send.at[step],
            recv_sem=top_recv.at[step], device_id=device_after(step), device_id_type=MESH)

    def start_report(step, carry):
        report(step).start()
        return carry

    def collect(step, best):
        report(step).wait_recv()
        return jnp.maximum(best, landing[step])

    def finish(step, carry):
        report(step).wait_send()
        return carry

    def finish_sends(step, carry):
        for copy in exchange(step, False):
            copy.wait_send()
        return carry

    lax.fori_loop(1, everyone, start_report, 0)
    lax.fori_loop(1, n, finish_sends, 0)
    best = lax.fori_loop(1, everyone, collect, top[...])
    lax.fori_loop(1, everyone, finish, 0)
    best_ref[...] = best[:, :LEAVES]


def body(bin_index, leaf_ids, gradients, hessians):
    n, n_feat = lax.axis_size("rows"), lax.axis_size("feat")
    rows, local_features = bin_index.shape
    own = local_features // n
    group = 2 if own % 2 == 0 else 1
    tiles = rows // LANES
    pieces = 4
    everyone = n * n_feat
    vmem = pl.BlockSpec(memory_space=pltpu.VMEM)
    dma = pltpu.SemaphoreType.DMA
    gain, best = pl.pallas_call(
        functools.partial(kernel, n, n_feat, group),
        out_shape=(jax.ShapeDtypeStruct((own, LEAVES, BINS), jnp.float32),
                   jax.ShapeDtypeStruct((1, LEAVES), jnp.float32)),
        in_specs=[pl.BlockSpec(memory_space=pl.ANY), vmem, vmem, vmem],
        out_specs=(vmem, vmem),
        scratch_shapes=[
            pltpu.VMEM((rows, local_features), jnp.int32),
            pltpu.VMEM((n, own, rows), jnp.bfloat16),
            pltpu.VMEM((3 * tiles, LANES), jnp.bfloat16),
            pltpu.VMEM((n, own, rows), jnp.bfloat16),
            pltpu.VMEM((n, 3 * tiles, LANES), jnp.bfloat16),
            pltpu.VMEM((2 * LEAVES, rows), jnp.bfloat16),
            pltpu.VMEM((own, 4 * LEAVES, HALF), jnp.float32),
            pltpu.VMEM((1, LANES), jnp.float32),
            pltpu.VMEM((everyone, 1, LANES), jnp.float32),
            dma((pieces,)), dma((n,)), dma((n,)), dma((n,)), dma((n,)), dma((2,)),
            dma((everyone,)), dma((everyone,)),
        ],
        compiler_params=pltpu.CompilerParams(
            collective_id=0, has_side_effects=True, vmem_limit_bytes=60 * 1024 * 1024),
    )(bin_index, leaf_ids.reshape(tiles, LANES), gradients.reshape(tiles, LANES), hessians.reshape(tiles, LANES))
    return gain[None], best.reshape(LEAVES)


def solution(mesh):
    placed = (P("rows", "feat"), P("rows"), P("rows"), P("rows"))
    return jax.shard_map(
        body,
        mesh=mesh,
        in_specs=placed,
        out_specs=(P("feat", "rows", None, None), P()),
        check_vma=False,
    )
```

time: 54 us -> 43 us (0.80)
  Pallas kernels: 46.5 us -> 39.9 us
  local copies, waits for them, and re-layouts: 4.69 us -> 2.19 us
  other arithmetic: 1.88 us -> 0 us
    pallas_call x1, Pallas kernels: 46.5 us -> 39.9 us  [body(): pl.pallas_call(functools.partial(kernel, n, n_feat, group), out_shape=(ja...]
    slice x1 -> x0, local copies, waits for them, and re-layouts: 1.32 us -> none  [body(): return (gain[None], best[:, 0])]
    convert_element_type x1 -> x0, other arithmetic: 1.28 us -> none  [body(): bins = bin_index.T.astype(jnp.bfloat16).reshape(n, own, rows)]
    convert_element_type x1 -> x0, local copies, waits for them, and re-layouts: 0.99 us -> none  [body(): bins = bin_index.T.astype(jnp.bfloat16).reshape(n, own, rows)]
    concatenate x2 -> x0, other arithmetic: 0.6 us -> none  [body(): jnp.concatenate([leaf_ids.astype(jnp.bfloat16), gradients, hessians])]
    unnamed x7 -> x4, local copies, waits for them, and re-layouts: 2.37 us -> 2.19 us
where the time goes in v2:
time: 43 us; the launch traced here: 42.8 us
  Pallas kernels  39.9 us (93%)
  local copies, waits for them, and re-layouts  2.19 us (5%)
  between operations  0.65 us (2%)
    pallas_call x1, Pallas kernels, body(): pl.pallas_call(functools.partial(kernel, n, n_feat, group), out_shape=(ja...  39.9 us
    unnamed x4, local copies, waits for them, and re-layouts  2.19 us

profile of v2, /device:TPU:0, one launch (start us, length us, event | category | flops | bytes accessed | tf_op | source)
XLA Modules:
  0.0 42.8 jit_solution(17045482632214105551)
XLA Ops:
  0.6 39.9 %shard_map.59 = (f32[16,16,256]{2,1,0:T(8,128)}, f32[1,16]{1,0:T(1,128)}) custom-call(s32[2048,128]{1,0:T(8,128)} %bins_hbm.1, s32[16,128]{1,0:T(8,128)} %bitcast.6, bf16[16,128]{1,0:T(8,128)(2,1)} %bitcast.7, bf16[16,128]{1,0:T(8,128)(2,1)} %bitcast.8), custom_call_target="tpu_custom_call" | custom-call | tf_op jit(solution)/shard_map/pallas_call | solution.py:193
  40.6 0.0 copy-start
  40.6 1.7 %copy.8 = f32[1,16,16,256]{3,2,1,0:T(8,128)} copy(f32[1,16,16,256]{3,2,1,0:T(8,128)} %bitcast.5) | data formatting | bytes 524288
  42.2 0.0 copy-done
  42.2 0.5 %copy.9 = f32[16]{0:T(128)} copy(f32[16]{0:T(128)S(1)} %bitcast.9) | data formatting | bytes 128
Async XLA Ops:
  40.6 1.7 %copy-start = (f32[1,16]{1,0:T(1,128)S(1)}, f32[1,16]{1,0:T(1,128)}, u32[]{:S(2)}) copy-start(f32[1,16]{1,0:T(1,128)} %get-tuple-element.5) | copy-start | bytes 196

commit v3 on v2

--- a/solution.py
+++ b/solution.py
@@ -16,8 +16,8 @@
 reg_lambda = 1.0
 
 
-def kernel(n, n_feat, group, bins_hbm, leaf_ref, grad_ref, hess_ref, gain_ref, best_ref,
-           raw, bins_src, meta_src, columns, metas, weights, sums, top, landing,
+def kernel(n, n_feat, group, bins_hbm, leaf_hbm, grad_hbm, hess_hbm, gain_ref, best_ref,
+           leaf_ref, grad_ref, hess_ref, small_sems, raw, bins_src, meta_src, columns, metas, weights, sums, top, landing,
            raw_sems, bin_send, bin_recv, meta_send, meta_recv, own_sems, top_send, top_recv):
     me, me_feat = lax.axis_index("rows"), lax.axis_index("feat")
     everyone = n * n_feat
@@ -31,8 +31,12 @@
         span = pl.ds(piece * piece_rows, piece_rows)
         return pltpu.make_async_copy(bins_hbm.at[span], raw.at[span], raw_sems.at[piece])
 
+    small = [pltpu.make_async_copy(source, target, small_sems.at[place]) for place, (source, target) in enumerate(
+        ((leaf_hbm, leaf_ref), (grad_hbm, grad_ref), (hess_hbm, hess_ref)))]
     for piece in range(pieces):
         fetch(piece).start()
+    for copy in small:
+        copy.start()
 
     def device_after(step):
         other = lax.rem(me_all + step, everyone)
@@ -46,6 +50,8 @@
 
     lax.fori_loop(1, everyone, greet, 0)
 
+    for copy in small:
+        copy.wait()
     meta_src[:tiles] = leaf_ref[...].astype(jnp.float32).astype(jnp.bfloat16)
     meta_src[tiles:2 * tiles] = grad_ref[...]
     meta_src[2 * tiles:] = hess_ref[...]
@@ -121,7 +127,7 @@
                 upper_wide = jnp.broadcast_to(bins, (2 * LEAVES, rows)) >= HALF
                 left_side.append(jnp.where(upper_wide, zero, table_rows))
                 left_side.append(jnp.where(upper_wide, table_rows, zero))
-                right_side.append(jnp.where(jnp.broadcast_to(low, (HALF, rows)) <= level, one, zero))
+                right_side.append(jnp.where(jnp.broadcast_to(low, (HALF, rows)) <= level, one, zero).astype(jnp.float8_e4m3fn))
             product = lax.dot_general(
                 jnp.concatenate(left_side, axis=0), jnp.concatenate(right_side, axis=0),
                 (((1,), (1,)), ((), ())), preferred_element_type=jnp.float32)
@@ -146,7 +152,7 @@
             largest = jnp.maximum(largest, gain)
         return largest
 
-    largest = lax.fori_loop(0, own, gains, jnp.full((LEAVES, HALF), -jnp.inf, jnp.float32))
+    largest = lax.fori_loop(0, own, gains, jnp.full((LEAVES, HALF), -jnp.inf, jnp.float32), unroll=True)
     largest = jnp.broadcast_to(jnp.max(largest, axis=1, keepdims=True), (LEAVES, LANES))
     on_lane = (lax.broadcasted_iota(jnp.int32, (LEAVES, LANES), 0) == lax.broadcasted_iota(jnp.int32, (LEAVES, LANES), 1))
     top[...] = jnp.max(jnp.where(on_lane, largest, -jnp.inf), axis=0, keepdims=True)
@@ -192,11 +198,15 @@
     dma = pltpu.SemaphoreType.DMA
     gain, best = pl.pallas_call(
         functools.partial(kernel, n, n_feat, group),
-        out_shape=(jax.ShapeDtypeStruct((own, LEAVES, BINS), jnp.float32),
-                   jax.ShapeDtypeStruct((1, LEAVES), jnp.float32)),
-        in_specs=[pl.BlockSpec(memory_space=pl.ANY), vmem, vmem, vmem],
+        out_shape=(pltpu.VMEM((own, LEAVES, BINS), jnp.float32),
+                   pltpu.VMEM((1, LEAVES), jnp.float32)),
+        in_specs=[pl.BlockSpec(memory_space=pl.ANY)] * 4,
         out_specs=(vmem, vmem),
         scratch_shapes=[
+            pltpu.VMEM((tiles, LANES), jnp.int32),
+            pltpu.VMEM((tiles, LANES), jnp.bfloat16),
+            pltpu.VMEM((tiles, LANES), jnp.bfloat16),
+            dma((3,)),
             pltpu.VMEM((rows, local_features), jnp.int32),
             pltpu.VMEM((n, own, rows), jnp.bfloat16),
             pltpu.VMEM((3 * tiles, LANES), jnp.bfloat16),

time: 43 us -> 31.3 us (0.73)
  Pallas kernels: 39.9 us -> 29.3 us
  local copies, waits for them, and re-layouts: 2.19 us -> 1.22 us
    pallas_call x1, Pallas kernels: 39.9 us -> 29.3 us  [body(): pl.pallas_call(functools.partial(kernel, n, n_feat, group), out_shape=(pl...]
    unnamed x4 -> x2, local copies, waits for them, and re-layouts: 2.19 us -> 1.22 us
where the time goes in v3:
time: 31.3 us; the launch traced here: 31.1 us
  Pallas kernels  29.3 us (94%)
  local copies, waits for them, and re-layouts  1.22 us (4%)
  between operations  0.64 us (2%)
    pallas_call x1, Pallas kernels, body(): pl.pallas_call(functools.partial(kernel, n, n_feat, group), out_shape=(pl...  29.3 us
    unnamed x2, local copies, waits for them, and re-layouts  1.22 us

profile of v3, /device:TPU:0, one launch (start us, length us, event | category | flops | bytes accessed | tf_op | source)
XLA Modules:
  0.0 31.1 jit_solution(7761218286315700508)
XLA Ops:
  0.6 29.3 %shard_map.59 = (f32[16,16,256]{2,1,0:T(8,128)S(1)}, f32[1,16]{1,0:T(1,128)S(1)}) custom-call(s32[2048,128]{1,0:T(8,128)} %bins_hbm.1, s32[16,128]{1,0:T(8,128)} %bitcast.7, bf16[16,128]{1,0:T(8,128)(2,1)} %bitcast.8, bf16[16,128]{1,0:T(8,128)(2,1)} %bitcast.9), custom_call_target="tpu_custom_call" | custom-call | tf_op jit(solution)/shard_map/pallas_call | solution.py:199
  29.9 0.7 %copy.8 = f32[1,16,16,256]{3,2,1,0:T(8,128)} copy(f32[1,16,16,256]{3,2,1,0:T(8,128)S(1)} %bitcast.5) | data formatting | bytes 524288
  30.6 0.5 %copy.9 = f32[16]{0:T(128)} copy(f32[16]{0:T(128)S(1)} %bitcast.6) | data formatting | bytes 128
